TPU v7x, 32 devices: a whole 2x2x4 slice. The times are simulated.
32 devices in a mesh: groups: 2 (over y), seq: 4 (over z), exp: 2 (over x), tp: 2 (over core).
Axes of the slice: x: 2, y: 2, z: 4, core: 2. Of those that a mesh axis runs over, the one named last changes fastest.
Arguments:
- attn_query: bfloat16 [2048, 1152], P(('groups', 'seq'), ('exp', 'tp')), parts along dimension 0, may hold values from -6 to 6
- fresh_keys: bfloat16 [2048, 1152], P(('groups', 'seq'), ('exp', 'tp')), parts along dimension 0, may hold values from -6 to 6
- fresh_values: bfloat16 [2048, 1152], P(('groups', 'seq'), ('exp', 'tp')), parts along dimension 0, may hold values from -6 to 6
- stale_keys: bfloat16 [2048, 1152], P(('groups', 'seq'), ('exp', 'tp')), parts along dimension 0, may hold values from -6 to 6
- stale_values: bfloat16 [2048, 1152], P(('groups', 'seq'), ('exp', 'tp')), parts along dimension 0, may hold values from -6 to 6
- block_flags: int32 [16], P(('groups', 'seq')), parts along dimension 0, may hold values 0 or 1
- moe_tokens: bfloat16 [4096, 1152], P(('groups', 'seq', 'exp', 'tp')), parts along dimension 0, may hold values from -6 to 6
- expert_ids: int32 [4096, 2], P(('groups', 'seq', 'exp', 'tp')), parts along dimension 0, may hold values from 0 to 3, all different within a row; in each aligned block of 128 rows (0 to 127, 128 to 255, ...) at most 80 rows name the same one
- gate_weights: float32 [4096, 2], P(('groups', 'seq', 'exp', 'tp')), parts along dimension 0, may hold values from 0.25 to 1
- up_weight: bfloat16 [4, 1152, 4608], P('seq', None, ('exp', 'tp')), may hold values from -0.1875 to 0.1875
- up_bias: float32 [4, 4608], P('seq', ('exp', 'tp')), may hold values from -3 to 3
- down_weight: bfloat16 [4, 4608, 1152], P('seq', ('exp', 'tp')), may hold values from -0.09375 to 0.09375
- down_bias: float32 [4, 1152], P('seq'), may hold values from -2 to 2
Outputs:
- attn_out: bfloat16 [2048, 1152], P(('groups', 'seq'), ('exp', 'tp')), parts along dimension 0
- moe_out: bfloat16 [4096, 1152], P(('groups', 'seq', 'exp', 'tp')), parts along dimension 0
There are 2 independent parts, one for each index of `groups`. A program takes and returns all parts, laid end to end along the dimension named above; an argument that names none is the same for every part. Nothing has to cross between parts.
Inputs may be any that keep to these rules, and one draw needn't show every extreme that they name: `expert_ids`: the 2 ids of a token differ. In the rows of one device no expert is named more than 80 times, and in every draw some expert is named exactly 80 times in some device's rows.
All inputs are finite; a program needn't handle non-finite values. No bound on the sum of `block_flags` on one device may be relied on, other than what follows from the above.
Results may differ from a plain program's by a relative error of at most 0.014.
Values may be sent and summed in bfloat16 or wider, within the bound.
A program may use at most 64 MiB of HBM per device.

v0:
```python
import math
import jax
import jax.numpy as jnp
from jax import lax
from jax.sharding import PartitionSpec as P

HD = 72


def over_all_2(share, axis, dim, apply):
    everything = lax.all_gather(share, axis, axis=dim, tiled=True)
    return apply(everything, jnp.int32(0))


def attention_part(attn_query, fresh_keys, fresh_values, stale_keys, stale_values, block_flags):
    length = attn_query.shape[0]
    heads_here = attn_query.shape[1] // HD
    row_flags = (jnp.repeat(block_flags, length // block_flags.shape[0]) == 1)[:, None]
    keys = jnp.where(row_flags, fresh_keys, stale_keys)
    values = jnp.where(row_flags, fresh_values, stale_values)
    queries = attn_query.reshape(length, heads_here, HD)
    scale = 1.0 / math.sqrt(HD)
    initial = (
        jnp.full((heads_here, length), -1e30, jnp.float32),
        jnp.zeros((heads_here, length), jnp.float32),
        jnp.zeros((heads_here, length, HD), jnp.float32),
    )
    carry = initial
    piece = (
        lax.all_gather(keys, "seq", axis=0, tiled=True),
        lax.all_gather(values, "seq", axis=0, tiled=True),
    )
    count = piece[0].shape[0]
    width = math.gcd(count, 512)
    key_blocks = piece[0].reshape(count // width, width, heads_here, HD)
    value_blocks = piece[1].reshape(count // width, width, heads_here, HD)

    def advance(state, blocks):
        highest, totals, weighted = state
        key_block, value_block = blocks
        scores = (
            jnp.einsum("qhd,khd->hqk", queries, key_block, preferred_element_type=jnp.float32)
            * scale
        )
        new_high = jnp.maximum(highest, jnp.max(scores, axis=-1))
        rescale = jnp.exp(highest - new_high)
        probs = jnp.exp(scores - new_high[:, :, None])
        totals = totals * rescale + jnp.sum(probs, axis=-1)
        weighted = weighted * rescale[:, :, None] + jnp.einsum(
            "hqk,khd->hqd",
            probs.astype(jnp.bfloat16),
            value_block,
            preferred_element_type=jnp.float32,
        )
        return ((new_high, totals, weighted), None)

    carry, unused = lax.scan(advance, carry, (key_blocks, value_blocks))
    highest, totals, weighted = carry
    mixed = weighted / totals[:, :, None]
    return jnp.transpose(mixed, (1, 0, 2)).reshape(length, heads_here * HD).astype(jnp.bfloat16)


def expert_part(moe_tokens, expert_ids, gate_weights, up_weight, up_bias, down_weight, down_bias):
    tokens_here, width = moe_tokens.shape
    choose = expert_ids.shape[1]
    number = lax.axis_size("seq") * up_weight.shape[0]
    capacity = 5 * tokens_here // (2 * number)
    flat_ids = expert_ids.reshape(-1)
    hits = (flat_ids[:, None] == jnp.arange(number, dtype=jnp.int32)[None, :]).astype(jnp.int32)
    before = jnp.cumsum(hits, axis=0) - hits
    place = jnp.sum(before * hits, axis=1)
    slot = flat_ids * capacity + place
    slot_pairs = slot.reshape(tokens_here, choose)
    table = jnp.sum(
        (
            slot_pairs[None, :, :] == jnp.arange(number * capacity, dtype=jnp.int32)[:, None, None]
        ).astype(jnp.int32),
        axis=-1,
    )
    buffer = jnp.dot(
        table.astype(jnp.bfloat16), moe_tokens, preferred_element_type=jnp.float32
    ).astype(jnp.bfloat16)
    buffer = buffer.reshape(number, capacity, width)
    received = lax.all_to_all(buffer, "seq", split_axis=0, concat_axis=0, tiled=True)
    sources = received.shape[0]
    count = received.shape[1]
    flat_rows = received.reshape(sources * count, width)
    chip_rows = lax.all_gather(flat_rows, "tp", axis=0, tiled=True)

    def project(piece):
        return jax.nn.gelu(
            jnp.dot(chip_rows, piece[0], preferred_element_type=jnp.float32) + piece[1]
        ).astype(jnp.bfloat16)

    hidden = over_all_2(
        (up_weight[0], up_bias[0][None, :].astype(jnp.bfloat16)),
        "exp",
        1,
        lambda piece, start: project((piece[0], piece[1].astype(jnp.float32))),
    )
    down_whole = lax.all_gather(down_weight[0], "exp", axis=0, tiled=True)
    summed = lax.psum_scatter(
        jnp.dot(hidden, down_whole, preferred_element_type=jnp.float32).astype(jnp.bfloat16),
        "tp",
        scatter_dimension=0,
        tiled=True,
    ).astype(jnp.float32)
    result = (summed + down_bias[0][None, :]).astype(jnp.bfloat16).reshape(sources, count, width)
    returned = lax.all_to_all(result, "seq", split_axis=0, concat_axis=0, tiled=True)
    flat_out = returned.reshape(number * capacity, width)
    picked = flat_out[slot].reshape(tokens_here, choose, width).astype(jnp.float32)
    combined = jnp.sum(picked * gate_weights[:, :, None], axis=1)
    return combined.astype(jnp.bfloat16)


def local(
    attn_query,
    fresh_keys,
    fresh_values,
    stale_keys,
    stale_values,
    block_flags,
    moe_tokens,
    expert_ids,
    gate_weights,
    up_weight,
    up_bias,
    down_weight,
    down_bias,
):
    attn_out = attention_part(
        attn_query, fresh_keys, fresh_values, stale_keys, stale_values, block_flags
    )
    moe_out = expert_part(
        moe_tokens, expert_ids, gate_weights, up_weight, up_bias, down_weight, down_bias
    )
    return (attn_out, moe_out)


def solution(mesh):
    in_specs = (
        P(("groups", "seq"), ("exp", "tp")),
        P(("groups", "seq"), ("exp", "tp")),
        P(("groups", "seq"), ("exp", "tp")),
        P(("groups", "seq"), ("exp", "tp")),
        P(("groups", "seq"), ("exp", "tp")),
        P(("groups", "seq")),
        P(("groups", "seq", "exp", "tp"), None),
        P(("groups", "seq", "exp", "tp"), None),
        P(("groups", "seq", "exp", "tp"), None),
        P("seq", None, ("exp", "tp")),
        P("seq", ("exp", "tp")),
        P("seq", ("exp", "tp"), None),
        P("seq", None),
    )
    out_specs = (P(("groups", "seq"), ("exp", "tp")), P(("groups", "seq", "exp", "tp"), None))
    return jax.shard_map(local, mesh=mesh, in_specs=in_specs, out_specs=out_specs, check_vma=False)
```

profile of v0, /device:TPU:0, one launch (start us, length us, event | category | flops | bytes accessed | tf_op | source)
XLA Modules:
  0.0 262.1 jit_solution(10440550585438227936)
XLA Ops:
  7.2 0.8 copy.32
  8.3 1.2 reduce-window.6
  10.6 25.3 %all_to_all.10 = bf16[4,80,1152]{2,1,0:T(8,128)(2,1)} all-to-all(bf16[4,80,1152]{2,1,0:T(8,128)(2,1)S(1)} %bitcast.82), channel_id=1, replica_groups=mesh['groups'=2,'seq'=4,'exp'=2,'tp'=2] {'seq'}, dimensions={0} | all-to-all | bytes 1474560 | tf_op jit(solution)/shard_map/all_to_all | solution.py:84
  36.0 0.7 all-gather.8.cloned.1.call-update
  37.5 4.4 %all_gather.22 = bf16[1,2304]{1,0:T(2,128)(2,1)S(1)} all-gather(bf16[1,1152]{1,0:T(2,128)(2,1)S(1)} %convert_element_type.61), channel_id=1, replica_groups=mesh['groups'=2,'seq'=4,'exp'=2,'tp'=2] {'exp'}, dimensions={1}, use_global_device_ids=true | all-gather | bytes 6912 | tf_op jit(solution)/shard_map/all_gather | solution.py:11
  41.9 3.0 %all-gather.6.cloned.1.call-done = bf16[640,1152]{1,0:T(8,128)(2,1)} async-done(((bf16[320,1152]{1,0:T(8,128)(2,1)}), bf16[640,1152]{1,0:T(8,128)(2,1)}) %all-gather.6.cloned.1.call-update) | async-done | bytes 1474576 | tf_op jit(solution)/shard_map/all_gather | solution.py:88
  44.9 72.0 %all-gather.8.cloned.1.call-done = bf16[1,1152,2304]{2,1,0:T(8,128)(2,1)} async-done(((bf16[1,1152,1152]{2,1,0:T(8,128)(2,1)}), bf16[1,1152,2304]{2,1,0:T(8,128)(2,1)}) %all-gather.8.cloned.1.call-update) | async-done | bytes 5308432 | tf_op jit(solution)/shard_map/all_gather | solution.py:11
  116.9 9.6 %fusion.22 = bf16[640,2304]{1,0:T(8,128)(2,1)} fusion(bf16[640,1152]{1,0:T(8,128)(2,1)} %all-gather.6.cloned.1.call-done, bf16[1,1152,2304]{2,1,0:T(8,128)(2,1)} %all-gather.8.cloned.1.call-done, f32[2304]{0:T(1024)S(1)} %convert_reduce_fusion.1), kind=kOutput, calls=%fused_computation.30 | convolution fusion | flops 3412131840 | bytes 9741312 | tf_op jit(solution)/shard_map/dot_general | solution.py:92
  126.5 61.3 %all-gather.10.cloned.1.call-done = bf16[1,2304,1152]{2,1,0:T(8,128)(2,1)} async-done(((bf16[1,1152,1152]{2,1,0:T(8,128)(2,1)}), bf16[1,2304,1152]{2,1,0:T(8,128)(2,1)}) %all-gather.10.cloned.1.call-update) | async-done | bytes 5308432 | tf_op jit(solution)/shard_map/all_gather | solution.py:101
  187.8 8.5 %fusion.29 = bf16[640,1152]{1,0:T(8,128)(2,1)} fusion(bf16[640,2304]{1,0:T(8,128)(2,1)} %fusion.22, bf16[1,2304,1152]{2,1,0:T(8,128)(2,1)} %all-gather.10.cloned.1.call-done), kind=kOutput, calls=%fused_computation.35 | convolution fusion | flops 3398123520 | bytes 9732096 | tf_op jit(solution)/shard_map/dot_general | solution.py:103
  196.5 16.5 %all_gather.18 = bf16[1024,288]{0,1:T(8,128)(2,1)S(1)} all-gather(bf16[256,288]{0,1:T(8,128)(2,1)S(1)} %get-tuple-element.101), channel_id=1, replica_groups=mesh['groups'=2,'seq'=4,'exp'=2,'tp'=2] {'seq'}, dimensions={0}, use_global_device_ids=true | all-gather | bytes 737280 | tf_op jit(solution)/shard_map/all_gather | solution.py:30
  213.5 0.9 copy.30
  214.4 16.1 %all_gather.19 = bf16[1024,288]{0,1:T(8,128)(2,1)S(1)} all-gather(bf16[256,288]{0,1:T(8,128)(2,1)S(1)} %get-tuple-element.100), channel_id=1, replica_groups=mesh['groups'=2,'seq'=4,'exp'=2,'tp'=2] {'seq'}, dimensions={0}, use_global_device_ids=true | all-gather | bytes 737280 | tf_op jit(solution)/shard_map/all_gather | solution.py:31
  230.9 0.9 copy.31
  231.9 2.1 add_convert_fusion
  234.0 4.9 %all-to-all-start.1 = ((bf16[4,80,1152]{2,1,0:T(8,128)(2,1)}), bf16[4,80,1152]{2,1,0:T(8,128)(2,1)S(1)}, u32[]{:S(2)}, u32[]{:S(2)}) async-start(bf16[4,80,1152]{2,1,0:T(8,128)(2,1)} %bitcast.10), calls=%async_computation.2 | async-start | bytes 1474560 | tf_op jit(solution)/shard_map/all_to_all | solution.py:109
  238.8 6.9 %while.15 = (s32[]{:T(128)}, f32[4,256]{1,0:T(4,128)S(1)}, f32[4,256]{1,0:T(4,128)S(1)}, f32[4,256,72]{1,2,0:T(8,128)S(1)}, bf16[2,512,4,72]{1,3,2,0:T(8,128)(2,...) while((s32[]{:T(128)}, f32[4,256]{1,0:T(4,128)S(1)}, ...), condition=%wide.region_3.4_spmd.clone, body=%wide.region_0.3_spmd.clone.sunk | while | flops 155415552 | bytes 7685225 | solution.py:57
  238.8 1.5 bitcast_reduce_fusion.2
  240.8 1.5 convolution_add_fusion.2
  242.3 1.5 bitcast_reduce_fusion.2
  244.2 1.5 convolution_add_fusion.2
  246.7 4.9 %all-to-all-done.1 = bf16[4,80,1152]{2,1,0:T(8,128)(2,1)S(1)} async-done(((bf16[4,80,1152]{2,1,0:T(8,128)(2,1)}), bf16[4,80,1152]{2,1,0:T(8,128)(2,1)S(1)}, u32[]{:S(2)}, u32[]{:S(2)}) %all-to-all-start.1) | async-done | bytes 737312 | tf_op jit(solution)/shard_map/all_to_all | solution.py:109
  251.6 1.3 gather_fusion
  253.4 2.2 multiply_reduce_fusion
  (66 shorter events, 5.6 us)
Async XLA Ops:
  7.2 3.1 %copy-start = (bf16[128,1152]{1,0:T(8,128)(2,1)S(1)}, bf16[128,1152]{1,0:T(8,128)(2,1)}, u32[]{:S(2)}) copy-start(bf16[128,1152]{1,0:T(8,128)(2,1)} %param.21) | copy-start | bytes 884740
  7.2 37.7 %all-gather.6.cloned.1.call-start = ((), (), s32[]{:S(2)}) async-start(), calls=%async_computation.3 | async-start | bytes 2211840 | tf_op jit(solution)/shard_map/all_gather | solution.py:88
  36.0 1.5 copy-start.5
  36.0 80.9 %all-gather.8.cloned.1.call-start = ((), (), s32[]{:S(2)}) async-start(), calls=%async_computation.5 | async-start | bytes 7962624 | tf_op jit(solution)/shard_map/all_gather | solution.py:11
  36.7 151.0 %all-gather.10.cloned.1.call-start = ((), (), s32[]{:S(2)}) async-start(), calls=%async_computation.6 | async-start | bytes 7962624 | tf_op jit(solution)/shard_map/all_gather | solution.py:101
  37.5 194.4 %reduce-scatter.2.cloned.1.call-start = ((), (), s32[]{:S(2)}) async-start(), calls=%async_computation.4 | async-start | bytes 2211840 | tf_op jit(solution)/shard_map/reduce_scatter | solution.py:102
  126.5 69.9 %copy-start.8 = (s32[2]{0:T(128)S(1)}, s32[2]{0:T(128)}, u32[]{:S(2)}) copy-start(s32[2]{0:T(128)} %param.20) | copy-start | bytes 28
  126.5 70.0 %copy-start.1 = (bf16[256,288]{0,1:T(8,128)(2,1)S(1)}, bf16[256,288]{0,1:T(8,128)(2,1)}, u32[]{:S(2)}) copy-start(bf16[256,288]{0,1:T(8,128)(2,1)} %param.17) | copy-start | bytes 442372
  126.5 70.0 %copy-start.2 = (bf16[256,288]{0,1:T(8,128)(2,1)S(1)}, bf16[256,288]{0,1:T(8,128)(2,1)}, u32[]{:S(2)}) copy-start(bf16[256,288]{0,1:T(8,128)(2,1)} %param.19) | copy-start | bytes 442372
  126.5 70.0 %copy-start.3 = (bf16[256,288]{0,1:T(8,128)(2,1)S(1)}, bf16[256,288]{0,1:T(8,128)(2,1)}, u32[]{:S(2)}) copy-start(bf16[256,288]{0,1:T(8,128)(2,1)} %param.16) | copy-start | bytes 442372
  126.5 70.0 %copy-start.4 = (bf16[256,288]{0,1:T(8,128)(2,1)S(1)}, bf16[256,288]{0,1:T(8,128)(2,1)}, u32[]{:S(2)}) copy-start(bf16[256,288]{0,1:T(8,128)(2,1)} %param.18) | copy-start | bytes 442372
  213.1 18.7 %copy-start.6 = (f32[1,1152]{1,0:T(1,128)S(1)}, f32[1,1152]{1,0:T(1,128)}, u32[]{:S(2)}) copy-start(f32[1,1152]{1,0:T(1,128)} %param.27) | copy-start | bytes 13828
  234.0 17.6 %all-to-all-start.1 = ((bf16[4,80,1152]{2,1,0:T(8,128)(2,1)}), bf16[4,80,1152]{2,1,0:T(8,128)(2,1)S(1)}, u32[]{:S(2)}, u32[]{:S(2)}) async-start(bf16[4,80,1152]{2,1,0:T(8,128)(2,1)} %bitcast.10), calls=%async_computation.2 | async-start | bytes 1474560 | tf_op jit(solution)/shard_map/all_to_all | solution.py:109
  238.8 7.0 %copy-start.7 = (f32[128,2]{0,1:T(2,128)S(1)}, f32[128,2]{0,1:T(2,128)}, u32[]{:S(2)}) copy-start(f32[128,2]{0,1:T(2,128)} %param.23) | copy-start | bytes 3076
Sparse Core Ops, SparseCore 0:
  36.1 8.7 all-gather.5
  46.4 70.4 all-gather.7
  118.5 69.2 all-gather.9
  196.5 8.9 reduce-scatter.1
where the time goes:
time: 263 us; the launch traced here: 262 us
  waiting for transfers between devices  143 us (54%)
  blocking collectives  62.3 us (24%)
  matrix products  24.4 us (9%)
  between operations  14 us (5%)
  other arithmetic  7.3 us (3%)
  local copies, waits for them, and re-layouts  6.41 us (2%)
  starting transfers between devices  5.02 us (2%)
    all_gather x1, waiting for transfers between devices, over_all_2(): everything = lax.all_gather(share, axis, axis=dim, tiled=True)  72 us
    all_gather x1, waiting for transfers between devices, expert_part(): down_whole = lax.all_gather(down_weight[0], 'exp', axis=0, tiled=True)  61.3 us
    all_to_all x1, blocking collectives, expert_part(): lax.all_to_all(buffer, 'seq', split_axis=0, concat_axis=0, tiled=True)  25.3 us
    all_gather x1, blocking collectives, attention_part(): lax.all_gather(keys, 'seq', axis=0, tiled=True)  16.5 us
    all_gather x1, blocking collectives, attention_part(): lax.all_gather(values, 'seq', axis=0, tiled=True)  16.1 us
    dot_general x1, matrix products, project(): jnp.dot(chip_rows, piece[0], preferred_element_type=jnp.float32) + piece[1]  9.57 us
    dot_general x1, matrix products, expert_part(): jnp.dot(hidden, down_whole, preferred_element_type=jnp.float32)  8.54 us
  transfers between devices with their start and end apart: 5, of which 4 were waited for; matrix products, arithmetic and copies ran while one was open for 8% of the time, Pallas kernels for 0%

commit v1 on v0

--- a/solution.py
+++ b/solution.py
@@ -5,6 +5,14 @@
 from jax.sharding import PartitionSpec as P
 
 HD = 72
+
+
+def gather_by_exchange(shard, axis, dim):
+    size = lax.axis_size(axis)
+    repeats = [size if d == dim else 1 for d in range(shard.ndim)]
+    return lax.all_to_all(
+        jnp.tile(shard, repeats), axis, split_axis=dim, concat_axis=dim, tiled=True
+    )
 
 
 def over_all_2(share, axis, dim, apply):
@@ -98,7 +106,7 @@
         1,
         lambda piece, start: project((piece[0], piece[1].astype(jnp.float32))),
     )
-    down_whole = lax.all_gather(down_weight[0], "exp", axis=0, tiled=True)
+    down_whole = gather_by_exchange(down_weight[0], "exp", 0)
     summed = lax.psum_scatter(
         jnp.dot(hidden, down_whole, preferred_element_type=jnp.float32).astype(jnp.bfloat16),
         "tp",

time: 263 us -> 240 us (0.913)
  waiting for transfers between devices: 143 us -> 17 us
  blocking collectives: 62.3 us -> 163 us
  matrix products: 24.4 us -> 18.1 us
  starting transfers between devices: 5.02 us -> 10.1 us
  local copies, waits for them, and re-layouts: 6.41 us -> 10.5 us
    all_gather x1, blocking collectives: 4.37 us -> 105 us  [over_all_2(): everything = lax.all_gather(share, axis, axis=dim, tiled=True)]
    all_gather x1, waiting for transfers between devices: 72 us -> 10.3 us  [over_all_2(): everything = lax.all_gather(share, axis, axis=dim, tiled=True)]
    all_gather x1 -> x0, waiting for transfers between devices: 61.3 us -> none  [expert_part(): down_whole = lax.all_gather(down_weight[0], 'exp', axis=0, tiled=True)]
    dot_general x1 -> x0, matrix products: 9.57 us -> none  [project(): jnp.dot(chip_rows, piece[0], preferred_element_type=jnp.float32) + piece[1]]
    all_to_all x0 -> x1, starting transfers between devices: none -> 6.33 us  [gather_by_exchange(): lax.all_to_all(jnp.tile(shard, repeats), axis, split_axis=dim, concat_axi...]
    dot_general x1, matrix products: 8.54 us -> 13.7 us  [expert_part(): jnp.dot(hidden, down_whole, preferred_element_type=jnp.float32)]
    all_gather x1, waiting for transfers between devices: 2.95 us -> 0.02 us  [expert_part(): chip_rows = lax.all_gather(flat_rows, 'tp', axis=0, tiled=True)]
    another operation x2 -> x3, local copies, waits for them, and re-layouts: 0.1 us -> 2.87 us  [the longest x1 2.77 us: gather_by_exchange(): jnp.tile(shard, repeats)]
  transfers between devices with their start and end apart: 5 -> 5, of which waited for: 4 -> 2; matrix products, arithmetic and copies ran while one was open for 8% -> 5% of each run, Pallas kernels for 0% -> 0%
where the time goes in v1:
time: 240 us
  blocking collectives  163 us (68%)
  matrix products  18.1 us (8%)
  waiting for transfers between devices  17 us (7%)
  between operations  14 us (6%)
  local copies, waits for them, and re-layouts  10.5 us (4%)
  starting transfers between devices  10.1 us (4%)
  other arithmetic  7.3 us (3%)
    all_gather x1, blocking collectives, over_all_2(): everything = lax.all_gather(share, axis, axis=dim, tiled=True)  105 us
    all_to_all x1, blocking collectives, expert_part(): lax.all_to_all(buffer, 'seq', split_axis=0, concat_axis=0, tiled=True)  25.6 us
    all_gather x1, blocking collectives, attention_part(): lax.all_gather(keys, 'seq', axis=0, tiled=True)  16.3 us
    all_gather x1, blocking collectives, attention_part(): lax.all_gather(values, 'seq', axis=0, tiled=True)  15.5 us
    dot_general x1, matrix products, expert_part(): jnp.dot(hidden, down_whole, preferred_element_type=jnp.float32)  13.7 us
    all_gather x1, waiting for transfers between devices, over_all_2(): everything = lax.all_gather(share, axis, axis=dim, tiled=True)  10.3 us
    all_to_all x1, starting transfers between devices, gather_by_exchange(): lax.all_to_all(jnp.tile(shard, repeats), axis, split_axis=dim, concat_axi...  6.33 us
    all_to_all x1, waiting for transfers between devices, expert_part(): lax.all_to_all(result, 'seq', split_axis=0, concat_axis=0, tiled=True)  5.94 us
  transfers between devices with their start and end apart: 5, of which 2 were waited for; matrix products, arithmetic and copies ran while one was open for 5% of the time, Pallas kernels for 0%

profile of v1, /device:TPU:0, one launch (start us, length us, event | category | flops | bytes accessed | tf_op | source)
XLA Modules:
  0.0 239.9 jit_solution(4334723350687874995)
XLA Ops:
  7.2 0.8 copy.32
  8.3 1.2 reduce-window.6
  10.7 25.6 %all_to_all.19 = bf16[4,80,1152]{2,1,0:T(8,128)(2,1)} all-to-all(bf16[4,80,1152]{2,1,0:T(8,128)(2,1)S(1)} %bitcast.81), channel_id=1, replica_groups=mesh['groups'=2,'seq'=4,'exp'=2,'tp'=2] {'seq'}, dimensions={0} | all-to-all | bytes 1474560 | tf_op jit(solution)/shard_map/all_to_all | solution.py:92
  36.3 0.7 all-gather.6.cloned.1.call-update
  37.0 2.8 %tile.9 = bf16[2,1152,1152]{2,1,0:T(8,128)(2,1)} broadcast(bf16[1152,1152]{1,0:T(8,128)(2,1)S(1)} %bitcast.82), dimensions={1,2} | broadcast | bytes 7962624 | tf_op jit(solution)/shard_map/tile | solution.py:14
  39.8 6.3 %all-to-all-start.1 = ((bf16[2,1152,1152]{2,1,0:T(8,128)(2,1)}), bf16[2,1152,1152]{2,1,0:T(8,128)(2,1)}, u32[]{:S(2)}, u32[]{:S(2)}) async-start(bf16[2,1152,1152]{2,1,0:T(8,128)(2,1)} %tile.9), calls=%async_computation.1 | async-start | bytes 10616832 | tf_op jit(solution)/shard_map/all_to_all | solution.py:13
  46.2 105.3 %all_gather.19 = bf16[1,2304]{1,0:T(2,128)(2,1)S(1)} all-gather(bf16[1,1152]{1,0:T(2,128)(2,1)S(1)} %convert_element_type.61), channel_id=1, replica_groups=mesh['groups'=2,'seq'=4,'exp'=2,'tp'=2] {'exp'}, dimensions={1}, use_global_device_ids=true | all-gather | bytes 6912 | tf_op jit(solution)/shard_map/all_gather | solution.py:19
  151.6 10.3 %all-gather.6.cloned.1.call-done = bf16[1,1152,2304]{2,1,0:T(8,128)(2,1)} async-done(((bf16[1,1152,1152]{2,1,0:T(8,128)(2,1)}), bf16[1,1152,2304]{2,1,0:T(8,128)(2,1)}) %all-gather.6.cloned.1.call-update) | async-done | bytes 5308432 | tf_op jit(solution)/shard_map/all_gather | solution.py:19
  161.9 13.7 %convolution_convert_fusion = bf16[640,1152]{1,0:T(8,128)(2,1)} fusion(bf16[2304,1152]{1,0:T(8,128)(2,1)} %bitcast.10, bf16[640,1152]{1,0:T(8,128)(2,1)} %all-gather.4.cloned.1.call-done, bf16[1,1152,2304]{2,1,0:T(8,128)(2,1)} %all-gather.6.cloned.1.call-done, f32[2304]{0:T(1024)S(1)} %convert_reduce_fusion.1), kind=kOutput, calls=%fused_computation.33 | convolution fusion | flops 6810255360 | bytes 13575168 | tf_op jit(solution)/shard_map/dot_general | solution.py:111
  175.8 16.3 %all_gather.15 = bf16[1024,288]{0,1:T(8,128)(2,1)S(1)} all-gather(bf16[256,288]{0,1:T(8,128)(2,1)S(1)} %get-tuple-element.101), channel_id=1, replica_groups=mesh['groups'=2,'seq'=4,'exp'=2,'tp'=2] {'seq'}, dimensions={0}, use_global_device_ids=true | all-gather | bytes 737280 | tf_op jit(solution)/shard_map/all_gather | solution.py:38
  192.5 0.9 copy.30
  193.4 15.5 %all_gather.16 = bf16[1024,288]{0,1:T(8,128)(2,1)S(1)} all-gather(bf16[256,288]{0,1:T(8,128)(2,1)S(1)} %get-tuple-element.100), channel_id=1, replica_groups=mesh['groups'=2,'seq'=4,'exp'=2,'tp'=2] {'seq'}, dimensions={0}, use_global_device_ids=true | all-gather | bytes 737280 | tf_op jit(solution)/shard_map/all_gather | solution.py:39
  209.4 0.9 copy.31
  210.3 2.1 add_convert_fusion
  212.4 3.7 %all-to-all-start.2 = ((bf16[4,80,1152]{2,1,0:T(8,128)(2,1)}), bf16[4,80,1152]{2,1,0:T(8,128)(2,1)S(1)}, u32[]{:S(2)}, u32[]{:S(2)}) async-start(bf16[4,80,1152]{2,1,0:T(8,128)(2,1)} %bitcast.11), calls=%async_computation.3 | async-start | bytes 1474560 | tf_op jit(solution)/shard_map/all_to_all | solution.py:117
  216.1 6.3 %while.15 = (s32[]{:T(128)}, f32[4,256]{1,0:T(4,128)S(1)}, f32[4,256]{1,0:T(4,128)S(1)}, f32[4,256,72]{1,2,0:T(8,128)S(1)}, bf16[2,512,4,72]{1,3,2,0:T(8,128)(2,...) while((s32[]{:T(128)}, f32[4,256]{1,0:T(4,128)S(1)}, ...), condition=%wide.region_3.4_spmd.clone, body=%wide.region_0.3_spmd.clone.sunk | while | flops 155415552 | bytes 10044041 | solution.py:65
  216.1 1.5 bitcast_reduce_fusion.2
  218.1 0.7 copy-done.1
  219.3 1.5 bitcast_reduce_fusion.2
  221.2 0.7 copy-done.1
  222.7 0.7 divide_convert_fusion
  223.4 5.9 %all-to-all-done.2 = bf16[4,80,1152]{2,1,0:T(8,128)(2,1)S(1)} async-done(((bf16[4,80,1152]{2,1,0:T(8,128)(2,1)}), bf16[4,80,1152]{2,1,0:T(8,128)(2,1)S(1)}, u32[]{:S(2)}, u32[]{:S(2)}) %all-to-all-start.2) | async-done | bytes 737312 | tf_op jit(solution)/shard_map/all_to_all | solution.py:117
  229.3 1.3 gather_fusion
  231.2 2.2 multiply_reduce_fusion
  (71 shorter events, 5.2 us)
Async XLA Ops:
  7.2 3.1 %copy-start = (bf16[128,1152]{1,0:T(8,128)(2,1)S(1)}, bf16[128,1152]{1,0:T(8,128)(2,1)}, u32[]{:S(2)}) copy-start(bf16[128,1152]{1,0:T(8,128)(2,1)} %param.21) | copy-start | bytes 884740
  7.2 144.4 %all-gather.4.cloned.1.call-start = ((), (), s32[]{:S(2)}) async-start(), calls=%async_computation.4 | async-start | bytes 2211840 | tf_op jit(solution)/shard_map/all_gather | solution.py:96
  10.6 26.4 %copy-start.2 = (bf16[1,1152,1152]{2,1,0:T(8,128)(2,1)S(1)}, bf16[1,1152,1152]{2,1,0:T(8,128)(2,1)}, u32[]{:S(2)}) copy-start(bf16[1,1152,1152]{2,1,0:T(8,128)(2,1)} %param.26) | copy-start | bytes 7962628
  36.2 125.6 %all-gather.6.cloned.1.call-start = ((), (), s32[]{:S(2)}) async-start(), calls=%async_computation.6 | async-start | bytes 7962624 | tf_op jit(solution)/shard_map/all_gather | solution.py:19
  39.8 6.4 %copy-start.7 = (f32[1,1152]{1,0:T(1,128)S(1)}, f32[1,1152]{1,0:T(1,128)}, u32[]{:S(2)}) copy-start(f32[1,1152]{1,0:T(1,128)} %param.25) | copy-start | bytes 13828
  39.8 111.8 %all-to-all-start.1 = ((bf16[2,1152,1152]{2,1,0:T(8,128)(2,1)}), bf16[2,1152,1152]{2,1,0:T(8,128)(2,1)}, u32[]{:S(2)}, u32[]{:S(2)}) async-start(bf16[2,1152,1152]{2,1,0:T(8,128)(2,1)} %tile.9), calls=%async_computation.1 | async-start | bytes 10616832 | tf_op jit(solution)/shard_map/all_to_all | solution.py:13
  46.1 164.2 %reduce-scatter.2.cloned.1.call-start = ((), (), s32[]{:S(2)}) async-start(), calls=%async_computation.5 | async-start | bytes 2211840 | tf_op jit(solution)/shard_map/reduce_scatter | solution.py:110
  161.8 13.8 %copy-start.10 = (s32[2]{0:T(128)S(1)}, s32[2]{0:T(128)}, u32[]{:S(2)}) copy-start(s32[2]{0:T(128)} %param.20) | copy-start | bytes 28
  161.8 13.9 %copy-start.3 = (bf16[256,288]{0,1:T(8,128)(2,1)S(1)}, bf16[256,288]{0,1:T(8,128)(2,1)}, u32[]{:S(2)}) copy-start(bf16[256,288]{0,1:T(8,128)(2,1)} %param.17) | copy-start | bytes 442372
  161.9 13.9 %copy-start.4 = (bf16[256,288]{0,1:T(8,128)(2,1)S(1)}, bf16[256,288]{0,1:T(8,128)(2,1)}, u32[]{:S(2)}) copy-start(bf16[256,288]{0,1:T(8,128)(2,1)} %param.19) | copy-start | bytes 442372
  161.9 13.9 %copy-start.5 = (bf16[256,288]{0,1:T(8,128)(2,1)S(1)}, bf16[256,288]{0,1:T(8,128)(2,1)}, u32[]{:S(2)}) copy-start(bf16[256,288]{0,1:T(8,128)(2,1)} %param.16) | copy-start | bytes 442372
  161.9 13.9 %copy-start.6 = (bf16[256,288]{0,1:T(8,128)(2,1)S(1)}, bf16[256,288]{0,1:T(8,128)(2,1)}, u32[]{:S(2)}) copy-start(bf16[256,288]{0,1:T(8,128)(2,1)} %param.18) | copy-start | bytes 442372
  192.5 17.8 %copy-start.8 = (f32[1,1152]{1,0:T(1,128)S(1)}, f32[1,1152]{1,0:T(1,128)}, u32[]{:S(2)}) copy-start(f32[1,1152]{1,0:T(1,128)} %param.27) | copy-start | bytes 13828
  212.4 16.9 %all-to-all-start.2 = ((bf16[4,80,1152]{2,1,0:T(8,128)(2,1)}), bf16[4,80,1152]{2,1,0:T(8,128)(2,1)S(1)}, u32[]{:S(2)}, u32[]{:S(2)}) async-start(bf16[4,80,1152]{2,1,0:T(8,128)(2,1)} %bitcast.11), calls=%async_computation.3 | async-start | bytes 1474560 | tf_op jit(solution)/shard_map/all_to_all | solution.py:117
  216.1 6.4 %copy-start.9 = (f32[128,2]{0,1:T(2,128)S(1)}, f32[128,2]{0,1:T(2,128)}, u32[]{:S(2)}) copy-start(f32[128,2]{0,1:T(2,128)} %param.23) | copy-start | bytes 3076
  217.7 1.1 copy-start.1
  220.8 1.1 copy-start.1
Sparse Core Ops, SparseCore 0:
  36.4 8.7 all-gather.3
  46.7 115.0 all-gather.5
  175.7 7.4 reduce-scatter.1
